TPU v7x, 32 devices: a whole 2x2x4 slice. The times are simulated.
32 devices in a mesh: dp: 8 (over z, y), seq: 4 (over x, core).
Axes of the slice: x: 2, y: 2, z: 4, core: 2. Of those that a mesh axis runs over, the one named last changes fastest.
Arguments:
- queries: bfloat16 [8, 512, 2048], P('dp', 'seq'), may hold values from -5 to 5
- keys: bfloat16 [8, 512, 2048], P('dp', 'seq'), may hold values from -5 to 5
- values: bfloat16 [8, 512, 2048], P('dp', 'seq'), may hold values from -6 to 6
- stream: bfloat16 [8, 512, 2048], P('dp', 'seq'), may hold values from -40 to 40
- layer_scale: float32 [2048], replicated, may hold values from 0.5 to 2
- norm_gain: float32 [2048], replicated, may hold values from 0.5 to 2
- teacher_gram: bfloat16 [8, 512, 512], P('dp', 'seq'), may hold values from -20 to 20, as said below
Outputs:
- feature_grad: bfloat16 [8, 512, 2048], P('dp', 'seq')
- image_loss: float32 [8], P('dp')
- mean_loss: float32 [], replicated
Inputs may be any that keep to these rules, and one draw needn't show every extreme that they name: Each image's teacher_gram is symmetric.
All inputs are finite; a program needn't handle non-finite values.
Results may differ from a plain program's by a relative error of at most 0.009.
Values may be sent and summed in bfloat16 or wider, within the bound.
A program may use at most 64 MiB of HBM per device.

v0:
```python
import math

import jax
import jax.numpy as jnp
from jax import lax
from jax.sharding import PartitionSpec as P

HEAD_DIM = 64


EPSILON = 1e-06


def attend_block(q_block, k_head, v_head):
    scores = jnp.einsum(
        "qd,kd->qk", q_block, k_head, preferred_element_type=jnp.float32
    ) / math.sqrt(q_block.shape[1])
    row_max = jnp.max(scores, axis=1, keepdims=True)
    exponent = jnp.exp(scores - row_max)
    weights = (exponent / jnp.sum(exponent, axis=1, keepdims=True)).astype(jnp.bfloat16)
    return jnp.dot(weights, v_head, preferred_element_type=jnp.float32).astype(jnp.bfloat16)


def attend_head(q_head, k_head, v_head):
    row_count, head_depth = q_head.shape
    block_rows = math.gcd(row_count, 512)
    blocks = q_head.reshape(row_count // block_rows, block_rows, head_depth)
    results = lax.map(lambda q_block: attend_block(q_block, k_head, v_head), blocks)
    return results.reshape(row_count, head_depth)


def forward_norm(summed, norm_gain):
    row_mean = jnp.mean(summed, axis=-1, keepdims=True)
    centred = summed - row_mean
    variance = jnp.mean(centred * centred, axis=-1, keepdims=True)
    inv_sigma = lax.rsqrt(variance + EPSILON)
    centred_hat = centred * inv_sigma
    normed = centred_hat * norm_gain
    inv_length = lax.rsqrt(jnp.sum(normed * normed, axis=-1, keepdims=True) + EPSILON)
    return (centred_hat, inv_sigma, normed, inv_length)


def backward_norm(cotangent, centred_hat, inv_sigma, normed, inv_length, norm_gain):
    along = jnp.sum(normed * cotangent, axis=-1, keepdims=True)
    grad_normed = inv_length * cotangent - inv_length * inv_length * inv_length * normed * along
    scaled = grad_normed * norm_gain
    mean_scaled = jnp.mean(scaled, axis=-1, keepdims=True)
    mean_product = jnp.mean(scaled * centred_hat, axis=-1, keepdims=True)
    return (scaled - mean_scaled - centred_hat * mean_product) * inv_sigma


def local(queries, keys, values, stream, layer_scale, norm_gain, teacher_gram):
    head_q, head_k, head_v = (
        lax.all_to_all(queries[0], "seq", split_axis=1, concat_axis=0, tiled=True),
        lax.all_to_all(keys[0], "seq", split_axis=1, concat_axis=0, tiled=True),
        lax.all_to_all(values[0], "seq", split_axis=1, concat_axis=0, tiled=True),
    )
    head_count = head_q.shape[1] // HEAD_DIM
    pieces = []
    for head_index in range(head_count):
        low_col = head_index * HEAD_DIM
        high_col = low_col + HEAD_DIM
        pieces.append(
            attend_head(
                head_q[:, low_col:high_col],
                head_k[:, low_col:high_col],
                head_v[:, low_col:high_col],
            )
        )
    attended_heads = jnp.concatenate(pieces, axis=1)
    attended = lax.all_to_all(attended_heads, "seq", split_axis=0, concat_axis=1, tiled=True)
    summed = stream[0].astype(jnp.float32) + layer_scale * attended.astype(jnp.float32)
    centred_hat, inv_sigma, normed, inv_length = forward_norm(summed, norm_gain)
    features = (normed * inv_length).astype(jnp.bfloat16)
    teacher_rows = teacher_gram[0]
    row_count, width_all = features.shape
    cycle_size = lax.axis_size("seq")
    tokens_all = row_count * cycle_size
    piece = lax.all_gather(features, "seq", axis=0, tiled=True)
    gram_tile = jnp.einsum("ad,bd->ab", features, piece, preferred_element_type=jnp.float32)
    taught = teacher_rows.astype(jnp.float32)
    differ = gram_tile - taught
    grad_acc = jnp.dot(differ.astype(jnp.bfloat16), piece, preferred_element_type=jnp.float32)
    loss_part = jnp.sum(differ * differ)
    loss_weight = width_all / (tokens_all * tokens_all)
    cotangent = grad_acc * (4.0 * width_all / (tokens_all * tokens_all))
    grad_summed = backward_norm(cotangent, centred_hat, inv_sigma, normed, inv_length, norm_gain)
    feature_grad = (grad_summed * (tokens_all * math.sqrt(width_all))).astype(jnp.bfloat16)[None]
    image_count = lax.axis_size("dp")
    image_total = lax.psum(loss_part, "seq")
    image_loss = image_total * loss_weight
    mean_loss = lax.psum(image_loss, "dp") / image_count
    return (feature_grad, jnp.reshape(image_loss, (1,)), mean_loss)


def solution(mesh):
    return jax.shard_map(
        local,
        mesh=mesh,
        in_specs=(
            P("dp", "seq", None),
            P("dp", "seq", None),
            P("dp", "seq", None),
            P("dp", "seq", None),
            P(),
            P(),
            P("dp", "seq", None),
        ),
        out_specs=(P("dp", "seq", None), P("dp"), P()),
        check_vma=False,
    )
```

profile of v0, /device:TPU:0, one launch (start us, length us, event | category | flops | bytes accessed | tf_op | source)
XLA Modules:
  0.0 143.6 jit_solution(15839510639580892488)
XLA Ops:
  7.2 2.1 %copy.19 = bf16[1,128,2048]{1,2,0:T(8,128)(2,1)} copy(bf16[1,128,2048]{2,1,0:T(8,128)(2,1)} %param.7) | data formatting | bytes 1048576 | tf_op args[0]
  9.3 4.2 %all-to-all-start = ((bf16[128,4,512]{0,2,1:T(8,128)(2,1)}), bf16[128,4,512]{0,2,1:T(8,128)(2,1)S(1)}, u32[]{:S(2)}, u32[]{:S(2)}) async-start(bf16[128,4,512]{0,2,1:T(8,128)(2,1)} %bitcast.1), calls=%async_computation | async-start | bytes 1048576 | tf_op jit(solution)/shard_map/all_to_all | solution.py:54
  13.5 1.0 copy.21
  14.5 7.8 %all-to-all-done = bf16[128,4,512]{0,2,1:T(8,128)(2,1)S(1)} async-done(((bf16[128,4,512]{0,2,1:T(8,128)(2,1)}), bf16[128,4,512]{0,2,1:T(8,128)(2,1)S(1)}, u32[]{:S(2)}, u32[]{:S(2)}) %all-to-all-start) | async-done | bytes 524320 | tf_op jit(solution)/shard_map/all_to_all | solution.py:54
  22.4 3.5 %all-to-all-start.1 = ((bf16[128,4,512]{0,2,1:T(8,128)(2,1)}), bf16[128,4,512]{0,2,1:T(8,128)(2,1)S(1)}, u32[]{:S(2)}, u32[]{:S(2)}) async-start(bf16[128,4,512]{0,2,1:T(8,128)(2,1)} %bitcast.4), calls=%async_computation.1 | async-start | bytes 1048576 | tf_op jit(solution)/shard_map/all_to_all | solution.py:55
  25.8 1.0 copy.23
  27.1 7.5 %all-to-all-done.1 = bf16[128,4,512]{0,2,1:T(8,128)(2,1)S(1)} async-done(((bf16[128,4,512]{0,2,1:T(8,128)(2,1)}), bf16[128,4,512]{0,2,1:T(8,128)(2,1)S(1)}, u32[]{:S(2)}, u32[]{:S(2)}) %all-to-all-start.1) | async-done | bytes 524320 | tf_op jit(solution)/shard_map/all_to_all | solution.py:55
  34.6 4.1 %all-to-all-start.2 = ((bf16[128,4,512]{0,2,1:T(8,128)(2,1)}), bf16[128,4,512]{0,2,1:T(8,128)(2,1)}, u32[]{:S(2)}, u32[]{:S(2)}) async-start(bf16[128,4,512]{0,2,1:T(8,128)(2,1)} %bitcast.7), calls=%async_computation.2 | async-start | bytes 1048576 | tf_op jit(solution)/shard_map/all_to_all | solution.py:56
  39.0 1.4 fusion.46
  40.4 1.3 fusion.45
  41.7 1.3 fusion.47
  43.0 1.4 fusion.48
  44.4 1.3 fusion.49
  45.6 1.4 fusion.50
  47.4 0.4 fusion.52
  47.8 1.2 copy.24
  49.0 1.4 fusion.9
  50.4 1.6 %fusion.1 = bf16[8,4,8,128]{3,2,1,0:T(8,128)(2,1)S(1)} fusion(f32[512,512]{0,1:T(8,128)} %get-tuple-element.103, f32[512]{0:T(512)S(1)} %fusion.9, f32[512]{0:T(512)S(1)} %get-tuple-element.102, bf16[512,512]{1,0:T(8,128)(2,1)S(1)} %bitcast.83), kind=kOutput, calls=%fused_computation.18 | convolution fusion | flops 34373632 | bytes 1249280 | tf_op jit(solution)/shard_map/while/body/eval_jaxpr/dot_general | solution.py:21
  52.6 0.9 copy-done.5
  54.0 0.9 copy-done.4
  55.5 0.9 copy-done.3
  56.9 0.9 copy-done.2
  59.5 11.8 %all_to_all.67 = bf16[4,128,512]{1,2,0:T(8,128)(2,1)S(1)} all-to-all(bf16[4,128,512]{1,2,0:T(8,128)(2,1)S(1)} %bitcast_dynamic-update-slice_fusion), channel_id=1, replica_groups=mesh['dp'=8,'seq'=4] {'seq'}, dimensions={0} | all-to-all | bytes 1048576 | tf_op jit(solution)/shard_map/all_to_all | solution.py:71
  71.8 0.6 copy-done.1
  73.5 0.9 multiply_convert_fusion.1
  74.5 23.7 %all-gather.2.cloned.1.call-done = bf16[512,2048]{1,0:T(8,128)(2,1)} async-done(((bf16[128,2048]{1,0:T(8,128)(2,1)}), bf16[512,2048]{1,0:T(8,128)(2,1)}) %all-gather.2.cloned.1.call-update) | async-done | bytes 2097168 | tf_op jit(solution)/shard_map/all_gather | solution.py:79
  98.2 3.4 %multiply_reduce_fusion.4 = (f32[]{:T(128)}, bf16[128,512]{1,0:T(8,128)(2,1)S(1)}) fusion(bf16[1,128,512]{2,1,0:T(8,128)(2,1)S(1)} %copy-done.10, bf16[128,2048]{1,0:T(8,128)(2,1)} %multiply_convert_fusion.1, bf16[512,2048]{1,0:T(8,128)(2,1)} %all-gather.2.cloned.1.call-done), kind=kOutput, calls=%fused_computation.60 | convolution fusion | flops 268763136 | bytes 2883588 | tf_op jit(solution)/shard_map/ad,bd->ab/dot_general | solution.py:80
  101.6 6.5 %psum.14 = f32[]{:T(128)} all-reduce(f32[]{:T(128)} %get-tuple-element.133), channel_id=1, replica_groups=mesh['dp'=8,'seq'=4] {'seq'}, use_global_device_ids=true, to_apply=%region_23.24 | all-reduce | flops 1 | bytes 8 | tf_op jit(solution)/shard_map/psum | solution.py:90
  108.7 22.7 %psum.15 = f32[]{:T(128)} all-reduce(f32[]{:T(128)} %mul.157), channel_id=1, replica_groups=mesh['dp'=8,'seq'=4] {'dp'}, use_global_device_ids=true, to_apply=%region_24.25 | all-reduce | flops 1 | bytes 8 | tf_op jit(solution)/shard_map/psum | solution.py:92
  131.4 0.6 multiply_reduce_fusion.1
  132.0 0.5 fusion.44
  132.5 1.4 fusion.16
  (56 shorter events, 6.1 us)
Async XLA Ops:
  7.2 6.4 %copy-start.7 = (bf16[1,128,2048]{2,1,0:T(8,128)(2,1)S(1)}, bf16[1,128,2048]{2,1,0:T(8,128)(2,1)}, u32[]{:S(2)}) copy-start(bf16[1,128,2048]{2,1,0:T(8,128)(2,1)} %param.8) | copy-start | bytes 1572868
  7.2 18.7 %copy-start.8 = (bf16[1,128,2048]{2,1,0:T(8,128)(2,1)S(1)}, bf16[1,128,2048]{2,1,0:T(8,128)(2,1)}, u32[]{:S(2)}) copy-start(bf16[1,128,2048]{2,1,0:T(8,128)(2,1)} %param.9) | copy-start | bytes 1572868
  9.3 13.1 %all-to-all-start = ((bf16[128,4,512]{0,2,1:T(8,128)(2,1)}), bf16[128,4,512]{0,2,1:T(8,128)(2,1)S(1)}, u32[]{:S(2)}, u32[]{:S(2)}) async-start(bf16[128,4,512]{0,2,1:T(8,128)(2,1)} %bitcast.1), calls=%async_computation | async-start | bytes 1048576 | tf_op jit(solution)/shard_map/all_to_all | solution.py:54
  22.4 12.3 %all-to-all-start.1 = ((bf16[128,4,512]{0,2,1:T(8,128)(2,1)}), bf16[128,4,512]{0,2,1:T(8,128)(2,1)S(1)}, u32[]{:S(2)}, u32[]{:S(2)}) async-start(bf16[128,4,512]{0,2,1:T(8,128)(2,1)} %bitcast.4), calls=%async_computation.1 | async-start | bytes 1048576 | tf_op jit(solution)/shard_map/all_to_all | solution.py:55
  34.6 13.1 %all-to-all-start.2 = ((bf16[128,4,512]{0,2,1:T(8,128)(2,1)}), bf16[128,4,512]{0,2,1:T(8,128)(2,1)}, u32[]{:S(2)}, u32[]{:S(2)}) async-start(bf16[128,4,512]{0,2,1:T(8,128)(2,1)} %bitcast.7), calls=%async_computation.2 | async-start | bytes 1048576 | tf_op jit(solution)/shard_map/all_to_all | solution.py:56
  38.8 59.4 %all-gather.2.cloned.1.call-start = ((), (), s32[]{:S(2)}) async-start(), calls=%async_computation.4 | async-start | bytes 2621440 | tf_op jit(solution)/shard_map/all_gather | solution.py:79
  50.4 1.7 %copy-start.6 = (f32[512,512]{0,1:T(8,128)S(1)}, f32[512,512]{0,1:T(8,128)}, u32[]{:S(2)}) copy-start(f32[512,512]{0,1:T(8,128)} %get-tuple-element.101) | copy-start | bytes 3145732
  52.3 1.2 copy-start.5
  53.7 1.2 copy-start.4
  55.1 1.2 copy-start.3
  56.5 1.2 copy-start.2
  71.4 1.0 copy-start.1
  71.4 1.0 copy-start.11
  72.4 0.7 copy-start.9
  73.1 25.1 %copy-start.10 = (bf16[1,128,512]{2,1,0:T(8,128)(2,1)S(1)}, bf16[1,128,512]{2,1,0:T(8,128)(2,1)}, u32[]{:S(2)}) copy-start(bf16[1,128,512]{2,1,0:T(8,128)(2,1)} %param.13) | copy-start | bytes 393220
  98.2 33.2 %copy-start = (bf16[512,2048]{1,0:T(8,128)(2,1)S(1)}, bf16[512,2048]{1,0:T(8,128)(2,1)}, u32[]{:S(2)}) copy-start(bf16[512,2048]{1,0:T(8,128)(2,1)} %all-gather.2.cloned.1.call-done) | copy-start | bytes 6291460
Sparse Core Ops, SparseCore 0:
  74.6 23.5 all-gather.1
where the time goes:
time: 144 us
  blocking collectives  41 us (28%)
  waiting for transfers between devices  39.1 us (27%)
  between operations  17.8 us (12%)
  matrix products  16.5 us (11%)
  starting transfers between devices  11.9 us (8%)
  local copies, waits for them, and re-layouts  10.7 us (7%)
  other arithmetic  6.59 us (5%)
    all_gather x1, waiting for transfers between devices, local(): piece = lax.all_gather(features, 'seq', axis=0, tiled=True)  23.7 us
    psum x1, blocking collectives, local(): mean_loss = lax.psum(image_loss, 'dp') / image_count  22.7 us
    all_to_all x1, blocking collectives, local(): lax.all_to_all(attended_heads, 'seq', split_axis=0, concat_axis=1, tiled=...  11.8 us
    dot_general x8, matrix products, attend_block(): jnp.einsum('qd,kd->qk', q_block, k_head, preferred_element_type=jnp.float32)  8.71 us
    unnamed x34, local copies, waits for them, and re-layouts  8.69 us
    all_to_all x1, waiting for transfers between devices, local(): lax.all_to_all(queries[0], 'seq', split_axis=1, concat_axis=0, tiled=True)  7.81 us
    all_to_all x1, waiting for transfers between devices, local(): lax.all_to_all(keys[0], 'seq', split_axis=1, concat_axis=0, tiled=True)  7.52 us
    psum x1, blocking collectives, local(): image_total = lax.psum(loss_part, 'seq')  6.49 us
  transfers between devices with their start and end apart: 4, of which 3 were waited for; matrix products, arithmetic and copies ran while one was open for 8% of the time, Pallas kernels for 0%

commit v1 on v0

v1 whole, which is shorter than its diff:
```python
import functools
import math

import jax
import jax.numpy as jnp
from jax import lax
from jax.experimental import pallas as pl
from jax.experimental.pallas import tpu as pltpu
from jax.sharding import PartitionSpec as P

HEAD_DIM = 64
EPSILON = 1e-06
LANES = 128
CORES = 2
MESH = pl.DeviceIdType.MESH
NT = (((1,), (1,)), ((), ()))
TN = (((0,), (0,)), ((), ()))


def kernel(
    seq_size,
    dp_size,
    chunk_count,
    slab_count,
    q_hbm,
    k_hbm,
    v_hbm,
    stream_hbm,
    scale_hbm,
    gain_hbm,
    teacher_hbm,
    grad_ref,
    image_ref,
    mean_ref,
    q_buf,
    kv_buf,
    stream_buf,
    scale_buf,
    gain_buf,
    teacher_buf,
    taught_t,
    hat_buf,
    feat_buf,
    cot_buf,
    stats,
    loss_acc,
    loss_seq,
    loss_dp,
    local_sem,
    kv_send,
    kv_recv,
    pair_send,
    pair_recv,
    relay_send,
    relay_recv,
    feat_send,
    feat_recv,
    fpair_send,
    fpair_recv,
    frelay_send,
    frelay_recv,
    lseq_send,
    lseq_recv,
    ldp_send,
    ldp_recv,
):
    rows, width = q_buf.shape
    chips = seq_size // CORES
    others = chips - 1
    tokens = rows * seq_size
    cols = width // chunk_count
    slab = rows // slab_count
    me = lax.axis_index("seq")
    image = lax.axis_index("dp")
    core = lax.rem(me, CORES)
    chip = me // CORES
    partner = chip * CORES + (1 - core)

    def far(d):
        return lax.rem(chip + d, chips) * CORES + core

    def source(d):
        return lax.rem(chip + chips - d, chips) * CORES + core

    def source_pair(d):
        return lax.rem(chip + chips - d, chips) * CORES + (1 - core)

    inputs = (k_hbm, v_hbm)
    locals_ = [
        pltpu.make_async_copy(src, dst, local_sem.at[i])
        for i, (src, dst) in enumerate(
            (
                (q_hbm.at[0], q_buf),
                (k_hbm.at[0], kv_buf.at[0, me]),
                (v_hbm.at[0], kv_buf.at[1, me]),
                (stream_hbm.at[0], stream_buf),
                (scale_hbm, scale_buf),
                (gain_hbm, gain_buf),
                (teacher_hbm.at[0], teacher_buf),
            )
        )
    ]

    barrier = pltpu.get_barrier_semaphore()

    def greet_seq(i, carry):
        pl.semaphore_signal(barrier, inc=1, device_id={"seq": lax.rem(me + i, seq_size)}, device_id_type=MESH)
        return carry

    def greet_dp(i, carry):
        pl.semaphore_signal(barrier, inc=1, device_id={"dp": lax.rem(image + i, dp_size)}, device_id_type=MESH)
        return carry

    lax.fori_loop(1, seq_size, greet_seq, 0)
    lax.fori_loop(1, dp_size, greet_dp, 0)
    for copy in locals_:
        copy.start()
    pl.semaphore_wait(barrier, seq_size + dp_size - 2)

    def span(j):
        return pl.ds(pl.multiple_of(j * cols, cols), cols)

    def direct(t, d, j):
        return pltpu.make_async_remote_copy(
            src_ref=inputs[t].at[0, :, span(j)],
            dst_ref=kv_buf.at[t, me, :, span(j)],
            send_sem=kv_send.at[t, d - 1],
            recv_sem=kv_recv.at[t, d - 1, j],
            device_id={"seq": far(d)},
            device_id_type=MESH,
        )

    def relay(t, d, j):
        block = kv_buf.at[t, source(d), :, span(j)]
        return pltpu.make_async_remote_copy(
            src_ref=block,
            dst_ref=block,
            send_sem=relay_send.at[t, d - 1],
            recv_sem=relay_recv.at[t, d - 1, j],
            device_id={"seq": partner},
            device_id_type=MESH,
        )

    def whole(t):
        return pltpu.make_async_remote_copy(
            src_ref=inputs[t].at[0],
            dst_ref=kv_buf.at[t, me],
            send_sem=pair_send.at[t],
            recv_sem=pair_recv.at[t],
            device_id={"seq": partner},
            device_id_type=MESH,
        )

    def send_chunk(j, carry):
        for d in range(1, chips):
            for t in range(2):
                direct(t, d, j).start()
        return carry

    send_chunk(0, 0)
    whole(0).start()
    whole(1).start()
    lax.fori_loop(1, chunk_count, send_chunk, 0)

    def relay_chunk(j):
        for d in range(1, chips):
            for t in range(2):
                direct(t, d, j).wait_recv()
                relay(t, d, j).start()

    for copy in locals_:
        copy.wait()
    for s in range(seq_size):
        taught_t[s * rows : (s + 1) * rows, :] = jnp.transpose(
            teacher_buf[:, s * rows : (s + 1) * rows].astype(jnp.float32)
        )
    cot_buf[...] = jnp.zeros_like(cot_buf)
    loss_acc[...] = jnp.zeros_like(loss_acc)

    heads = LANES // HEAD_DIM
    head_of_lane = lax.broadcasted_iota(jnp.int32, (rows, LANES), 1) // HEAD_DIM
    log2_scale = 1.0 / (math.sqrt(HEAD_DIM) * math.log(2.0))

    def attend(j):
        for d in range(1, chips):
            for t in range(2):
                relay(t, d, j).wait_recv()

        def group(p, carry):
            lanes = pl.ds(pl.multiple_of(j * cols + p * LANES, LANES), LANES)
            q = q_buf[:, lanes]
            stacked = jnp.concatenate(
                [jnp.where(head_of_lane == h, q, jnp.zeros_like(q)) for h in range(heads)], axis=0
            )
            k = kv_buf[0, :, :, lanes].reshape(tokens, LANES)
            v = kv_buf[1, :, :, lanes].reshape(tokens, LANES)
            scores = lax.dot_general(stacked, k, NT, preferred_element_type=jnp.float32)
            top = jnp.max(scores, axis=1, keepdims=True)
            weights = jnp.exp2((scores - top) * log2_scale)
            total = jnp.sum(weights, axis=1, keepdims=True)
            mixed = jnp.dot(weights.astype(jnp.bfloat16), v, preferred_element_type=jnp.float32)
            mixed = mixed * (1.0 / total)
            attended = mixed[:rows]
            for h in range(1, heads):
                attended = jnp.where(head_of_lane == h, mixed[h * rows : (h + 1) * rows], attended)
            attended = attended.astype(jnp.bfloat16).astype(jnp.float32)
            hat_buf[:, lanes] = stream_buf[:, lanes].astype(jnp.float32) + scale_buf[:, lanes] * attended
            return carry

        lax.fori_loop(0, cols // LANES, group, 0)

    relay_chunk(0)
    for t in range(2):
        whole(t).wait_recv()

    def attention_step(j, carry):
        relay_chunk(j)
        attend(j - 1)
        return carry

    lax.fori_loop(1, chunk_count, attention_step, 0)
    attend(chunk_count - 1)

    def part(r):
        return pl.ds(pl.multiple_of(r * slab, slab), slab)

    def fdirect(d, r):
        return pltpu.make_async_remote_copy(
            src_ref=feat_buf.at[me, part(r)],
            dst_ref=feat_buf.at[me, part(r)],
            send_sem=feat_send.at[d - 1, r],
            recv_sem=feat_recv.at[d - 1, r],
            device_id={"seq": far(d)},
            device_id_type=MESH,
        )

    def fpair(r):
        return pltpu.make_async_remote_copy(
            src_ref=feat_buf.at[me, part(r)],
            dst_ref=feat_buf.at[me, part(r)],
            send_sem=fpair_send.at[r],
            recv_sem=fpair_recv.at[r],
            device_id={"seq": partner},
            device_id_type=MESH,
        )

    def frelay(d, r):
        block = feat_buf.at[source(d), part(r)]
        return pltpu.make_async_remote_copy(
            src_ref=block,
            dst_ref=block,
            send_sem=frelay_send.at[d - 1, r],
            recv_sem=frelay_recv.at[d - 1, r],
            device_id={"seq": partner},
            device_id_type=MESH,
        )

    gain = gain_buf[...]

    def norm_slab(r, carry):
        here = part(r)
        summed = hat_buf[here, :]
        centred = summed - jnp.mean(summed, axis=1, keepdims=True)
        variance = jnp.mean(centred * centred, axis=1, keepdims=True)
        inv_sigma = lax.rsqrt(variance + EPSILON)
        hat = centred * inv_sigma
        normed = hat * gain
        inv_length = lax.rsqrt(jnp.sum(normed * normed, axis=1, keepdims=True) + EPSILON)
        feat_buf[me, here, :] = (normed * inv_length).astype(jnp.bfloat16)
        for d in range(1, chips):
            fdirect(d, r).start()
        fpair(r).start()
        hat_buf[here, :] = hat
        stats[0, here, :] = inv_sigma
        stats[1, here, :] = inv_length
        stats[2, here, :] = jnp.sum(normed * gain, axis=1, keepdims=True)
        return carry

    lax.fori_loop(0, slab_count, norm_slab, 0)

    def gram(s, start, size):
        block = feat_buf[s, pl.ds(start, size), :]
        tile = lax.dot_general(block, feat_buf[me], NT, preferred_element_type=jnp.float32)
        differ = tile - taught_t[pl.ds(pl.multiple_of(s * rows + start, size), size), :]
        loss_acc[...] += jnp.sum((differ * differ).reshape(size // 8, 8, rows), axis=0)
        cot_buf[...] += lax.dot_general(
            differ.astype(jnp.bfloat16), block, TN, preferred_element_type=jnp.float32
        )

    gram(me, 0, rows)
    for r in range(slab_count):
        fpair(r).wait_recv()
    gram(partner, 0, rows)

    def gram_step(i, carry):
        r = i // others
        d = lax.rem(i, others) + 1
        fdirect(d, r).wait_recv()
        frelay(d, r).start()
        start = pl.multiple_of(r * slab, slab)
        gram(source(d), start, slab)
        frelay(d, r).wait_recv()
        gram(source_pair(d), start, slab)
        return carry

    lax.fori_loop(0, others * slab_count, gram_step, 0)

    def lseq(i):
        return pltpu.make_async_remote_copy(
            src_ref=loss_seq.at[me],
            dst_ref=loss_seq.at[me],
            send_sem=lseq_send.at[i - 1],
            recv_sem=lseq_recv.at[i - 1],
            device_id={"seq": lax.rem(me + i, seq_size)},
            device_id_type=MESH,
        )

    def ldp(i):
        return pltpu.make_async_remote_copy(
            src_ref=loss_dp.at[image],
            dst_ref=loss_dp.at[image],
            send_sem=ldp_send.at[i - 1],
            recv_sem=ldp_recv.at[i - 1],
            device_id={"dp": lax.rem(image + i, dp_size)},
            device_id_type=MESH,
        )

    loss_seq[me] = loss_acc[...]
    for i in range(1, seq_size):
        lseq(i).start()

    inv_sigma = stats[0]
    inv_length = stats[1]
    cot_weight = 4.0 * width / (tokens * tokens)
    cot = cot_buf[...]
    along = cot_weight * jnp.sum(hat_buf[...] * gain * cot, axis=1, keepdims=True)
    gain_sum = cot_weight * jnp.sum(gain * cot, axis=1, keepdims=True)
    cubed = inv_length * inv_length * inv_length * along
    mean_scaled = (inv_length * gain_sum - cubed * stats[2]) * (1.0 / width)
    mean_product = cubed * (EPSILON / width)

    for i in range(1, seq_size):
        lseq(i).wait_recv()
    image_sum = loss_seq[0]
    for s in range(1, seq_size):
        image_sum = image_sum + loss_seq[s]
    loss_dp[image] = image_sum
    for i in range(1, dp_size):
        ldp(i).start()

    out_scale = inv_sigma * (tokens * math.sqrt(width))
    hat = hat_buf[...]
    scaled = (cot * (inv_length * cot_weight) - cubed * (hat * gain)) * gain
    grad_ref[0] = ((scaled - mean_scaled - hat * mean_product) * out_scale).astype(jnp.bfloat16)

    for i in range(1, dp_size):
        ldp(i).wait_recv()
    all_sum = loss_dp[0]
    for s in range(1, dp_size):
        all_sum = all_sum + loss_dp[s]
    loss_weight = width / (tokens * tokens)
    image_ref[0, 0] = jnp.sum(image_sum) * loss_weight
    mean_ref[0, 0] = jnp.sum(all_sum) * (loss_weight / dp_size)

    for t in range(2):
        whole(t).wait_send()
        for d in range(1, chips):
            pltpu.make_async_copy(inputs[t].at[0], kv_buf.at[t, me], kv_send.at[t, d - 1]).wait()
            pltpu.make_async_copy(inputs[t].at[0], kv_buf.at[t, me], relay_send.at[t, d - 1]).wait()
    for r in range(slab_count):
        fpair(r).wait_send()
        for d in range(1, chips):
            fdirect(d, r).wait_send()
            frelay(d, r).wait_send()
    for i in range(1, seq_size):
        lseq(i).wait_send()
    for i in range(1, dp_size):
        ldp(i).wait_send()


def local(seq_size, dp_size, queries, keys, values, stream, layer_scale, norm_gain, teacher_gram):
    rows, width = queries.shape[1:]
    others = max(1, seq_size // CORES - 1)
    tokens = rows * seq_size
    groups = width // LANES
    chunk_count = math.gcd(groups, max(1, 64 // seq_size))
    slab_count = max(1, rows // 32)
    dma = pltpu.SemaphoreType.DMA
    any_space = pl.BlockSpec(memory_space=pl.ANY)
    grad, image_loss, mean_loss = pl.pallas_call(
        functools.partial(kernel, seq_size, dp_size, chunk_count, slab_count),
        out_shape=(
            jax.ShapeDtypeStruct((1, rows, width), jnp.bfloat16),
            jax.ShapeDtypeStruct((1, 1), jnp.float32),
            jax.ShapeDtypeStruct((1, 1), jnp.float32),
        ),
        in_specs=[any_space] * 7,
        out_specs=(
            pl.BlockSpec(memory_space=pltpu.VMEM),
            pl.BlockSpec(memory_space=pltpu.SMEM),
            pl.BlockSpec(memory_space=pltpu.SMEM),
        ),
        scratch_shapes=[
            pltpu.VMEM((rows, width), jnp.bfloat16),
            pltpu.VMEM((2, seq_size, rows, width), jnp.bfloat16),
            pltpu.VMEM((rows, width), jnp.bfloat16),
            pltpu.VMEM((1, width), jnp.float32),
            pltpu.VMEM((1, width), jnp.float32),
            pltpu.VMEM((rows, tokens), jnp.bfloat16),
            pltpu.VMEM((tokens, rows), jnp.float32),
            pltpu.VMEM((rows, width), jnp.float32),
            pltpu.VMEM((seq_size, rows, width), jnp.bfloat16),
            pltpu.VMEM((rows, width), jnp.float32),
            pltpu.VMEM((3, rows, 1), jnp.float32),
            pltpu.VMEM((8, rows), jnp.float32),
            pltpu.VMEM((seq_size, 8, rows), jnp.float32),
            pltpu.VMEM((dp_size, 8, rows), jnp.float32),
            dma((7,)),
            dma((2, others)),
            dma((2, others, chunk_count)),
            dma((2,)),
            dma((2,)),
            dma((2, others)),
            dma((2, others, chunk_count)),
            dma((others, slab_count)),
            dma((others, slab_count)),
            dma((slab_count,)),
            dma((slab_count,)),
            dma((others, slab_count)),
            dma((others, slab_count)),
            dma((seq_size - 1,)),
            dma((seq_size - 1,)),
            dma((dp_size - 1,)),
            dma((dp_size - 1,)),
        ],
        compiler_params=pltpu.CompilerParams(
            collective_id=0, has_side_effects=True, vmem_limit_bytes=60 * 1024 * 1024
        ),
    )(
        queries,
        keys,
        values,
        stream,
        layer_scale.reshape(1, width),
        norm_gain.reshape(1, width),
        teacher_gram,
    )
    return grad, image_loss.reshape(1), mean_loss.reshape(())


def solution(mesh):
    return jax.shard_map(
        functools.partial(local, mesh.shape["seq"], mesh.shape["dp"]),
        mesh=mesh,
        in_specs=(
            P("dp", "seq", None),
            P("dp", "seq", None),
            P("dp", "seq", None),
            P("dp", "seq", None),
            P(),
            P(),
            P("dp", "seq", None),
        ),
        out_specs=(P("dp", "seq", None), P("dp"), P()),
        check_vma=False,
    )
```

time: 144 us -> 61 us (0.42)
  Pallas kernels: 0 us -> 54.8 us
  blocking collectives: 41 us -> 0 us
  waiting for transfers between devices: 39.1 us -> 0 us
  matrix products: 16.5 us -> 0 us
  between operations: 17.8 us -> 4.1 us
  starting transfers between devices: 11.9 us -> 0 us
  local copies, waits for them, and re-layouts: 10.7 us -> 1.88 us
  other arithmetic: 6.59 us -> 0 us
    pallas_call x0 -> x1, Pallas kernels: none -> 54.8 us  [local(): pl.pallas_call(functools.partial(kernel, seq_size, dp_size, chunk_count,...]
    psum x2 -> x0, blocking collectives: 29.2 us -> none  [the longest x1 22.7 us: local(): mean_loss = lax.psum(image_loss, 'dp') / image_count]
    all_gather x1 -> x0, waiting for transfers between devices: 23.7 us -> none  [local(): piece = lax.all_gather(features, 'seq', axis=0, tiled=True)]
    dot_general x18 -> x0, matrix products: 16.5 us -> none  [the longest x8 8.71 us: attend_block(): jnp.einsum('qd,kd->qk', q_block, k_head, preferred_element_type=jnp.float32)]
    all_to_all x3 -> x0, waiting for transfers between devices: 15.3 us -> none  [the longest x1 7.81 us: local(): lax.all_to_all(queries[0], 'seq', split_axis=1, concat_axis=0, tiled=True)]
    all_to_all x3 -> x0, starting transfers between devices: 11.8 us -> none  [the longest x1 4.24 us: local(): lax.all_to_all(queries[0], 'seq', split_axis=1, concat_axis=0, tiled=True)]
    all_to_all x1 -> x0, blocking collectives: 11.8 us -> none  [local(): lax.all_to_all(attended_heads, 'seq', split_axis=0, concat_axis=1, tiled=...]
    unnamed x34 -> x1, local copies, waits for them, and re-layouts: 8.69 us -> 1.88 us
  transfers between devices with their start and end apart: 4 -> 0, of which waited for: 3 -> 0; matrix products, arithmetic and copies ran while one was open for 8% -> 0% of each run, Pallas kernels for 0% -> 0%
where the time goes in v1:
time: 61 us; the launch traced here: 60.8 us
  Pallas kernels  54.8 us (90%)
  between operations  4.1 us (7%)
  local copies, waits for them, and re-layouts  1.88 us (3%)
    pallas_call x1, Pallas kernels, local(): pl.pallas_call(functools.partial(kernel, seq_size, dp_size, chunk_count,...  54.8 us
    unnamed x1, local copies, waits for them, and re-layouts  1.88 us

profile of v1, /device:TPU:0, one launch (start us, length us, event | category | flops | bytes accessed | tf_op | source)
XLA Modules:
  0.0 60.8 jit_solution(15064326841165156755)
XLA Ops:
  0.6 54.8 %shard_map.94 = (bf16[1,128,2048]{2,1,0:T(8,128)(2,1)}, f32[1,1]{1,0:T(1,128)}, f32[1,1]{1,0:T(1,128)}) custom-call(bf16[1,128,2048]{2,1,0:T(8,128)(2,1)} %q_hbm.1, bf16[1,128,2048]{2,1,0:T(8,128)(2,1)} %k_hbm.1, bf16[1,128,2048]{2,1,0:T(8,128)(2,1)} %v_hbm.1, bf16[1,128,2048]{2,1,0:T(8,128)(2,1)} %stream_hbm.1, f32[1,2048]{1,0:T(1,128)} %bitcast.4, ...), custom_call_target="tpu_custom_call" | custom-call | tf_op jit(solution)/shard_map/pallas_call | solution.py:390
  55.5 1.9 %copy.13 = bf16[1,128,2048]{2,1,0:T(8,128)(2,1)} copy(bf16[1,128,2048]{2,1,0:T(8,128)(2,1)} %get-tuple-element.12) | data formatting | bytes 1048576

commit v2 on v1

--- a/solution.py
+++ b/solution.py
@@ -44,8 +44,8 @@
     cot_buf,
     stats,
     loss_acc,
-    loss_seq,
-    loss_dp,
+    loss_all,
+    grad_buf,
     local_sem,
     kv_send,
     kv_recv,
@@ -59,10 +59,10 @@
     fpair_recv,
     frelay_send,
     frelay_recv,
-    lseq_send,
-    lseq_recv,
-    ldp_send,
-    ldp_recv,
+    loss_send,
+    loss_recv,
+    grad_sem,
+    ready,
 ):
     rows, width = q_buf.shape
     chips = seq_size // CORES
@@ -107,15 +107,19 @@
         pl.semaphore_signal(barrier, inc=1, device_id={"seq": lax.rem(me + i, seq_size)}, device_id_type=MESH)
         return carry
 
-    def greet_dp(i, carry):
-        pl.semaphore_signal(barrier, inc=1, device_id={"dp": lax.rem(image + i, dp_size)}, device_id_type=MESH)
-        return carry
-
     lax.fori_loop(1, seq_size, greet_seq, 0)
-    lax.fori_loop(1, dp_size, greet_dp, 0)
+    bits = dp_size.bit_length() - 1
+    cube = dp_size == 1 << bits
+
+    def across(k):
+        return image + (1 << k) * (1 - 2 * lax.rem(image // (1 << k), 2))
+
+    greeted = [across(k) for k in range(bits)] if cube else [lax.rem(image + i, dp_size) for i in range(1, dp_size)]
+    for peer in greeted:
+        pl.semaphore_signal(barrier, inc=1, device_id={"dp": peer}, device_id_type=MESH)
     for copy in locals_:
         copy.start()
-    pl.semaphore_wait(barrier, seq_size + dp_size - 2)
+    pl.semaphore_wait(barrier, seq_size - 1 + len(greeted))
 
     def span(j):
         return pl.ds(pl.multiple_of(j * cols, cols), cols)
@@ -161,6 +165,11 @@
     whole(0).start()
     whole(1).start()
     lax.fori_loop(1, chunk_count, send_chunk, 0)
+
+    if cube:
+        for k in range(bits):
+            pl.semaphore_signal(ready.at[k], inc=1, device_id={"dp": across(k)}, device_id_type=MESH)
+            pl.semaphore_wait(ready.at[k], 1)
 
     def relay_chunk(j):
         for d in range(1, chips):
@@ -283,51 +292,59 @@
         tile = lax.dot_general(block, feat_buf[me], NT, preferred_element_type=jnp.float32)
         differ = tile - taught_t[pl.ds(pl.multiple_of(s * rows + start, size), size), :]
         loss_acc[...] += jnp.sum((differ * differ).reshape(size // 8, 8, rows), axis=0)
-        cot_buf[...] += lax.dot_general(
-            differ.astype(jnp.bfloat16), block, TN, preferred_element_type=jnp.float32
-        )
-
-    gram(me, 0, rows)
+        return differ.astype(jnp.bfloat16)
+
+    def pull(differ, s, start, size):
+        block = feat_buf[s, pl.ds(start, size), :]
+        cot_buf[...] += lax.dot_general(differ, block, TN, preferred_element_type=jnp.float32)
+
+    pull(gram(me, 0, rows), me, 0, rows)
     for r in range(slab_count):
         fpair(r).wait_recv()
-    gram(partner, 0, rows)
-
-    def gram_step(i, carry):
+    pull(gram(partner, 0, rows), partner, 0, rows)
+
+    def gram_step(i, finish):
         r = i // others
         d = lax.rem(i, others) + 1
         fdirect(d, r).wait_recv()
         frelay(d, r).start()
         start = pl.multiple_of(r * slab, slab)
-        gram(source(d), start, slab)
+        pull(gram(source(d), start, slab), source(d), start, slab)
         frelay(d, r).wait_recv()
-        gram(source_pair(d), start, slab)
+        last = gram(source_pair(d), start, slab)
+        finish()
+        pull(last, source_pair(d), start, slab)
+
+    def plain_step(i, carry):
+        gram_step(i, lambda: None)
         return carry
 
-    lax.fori_loop(0, others * slab_count, gram_step, 0)
-
-    def lseq(i):
-        return pltpu.make_async_remote_copy(
-            src_ref=loss_seq.at[me],
-            dst_ref=loss_seq.at[me],
-            send_sem=lseq_send.at[i - 1],
-            recv_sem=lseq_recv.at[i - 1],
-            device_id={"seq": lax.rem(me + i, seq_size)},
-            device_id_type=MESH,
-        )
-
-    def ldp(i):
-        return pltpu.make_async_remote_copy(
-            src_ref=loss_dp.at[image],
-            dst_ref=loss_dp.at[image],
-            send_sem=ldp_send.at[i - 1],
-            recv_sem=ldp_recv.at[i - 1],
-            device_id={"dp": lax.rem(image + i, dp_size)},
-            device_id_type=MESH,
-        )
-
-    loss_seq[me] = loss_acc[...]
-    for i in range(1, seq_size):
-        lseq(i).start()
+    everyone = seq_size * dp_size
+    mine = image * seq_size + me
+
+    def send_loss():
+        loss_all[mine] = jnp.sum(loss_acc[...], axis=0, keepdims=True)
+
+        def tell(i, carry):
+            target = lax.rem(mine + i, everyone)
+            pltpu.make_async_remote_copy(
+                src_ref=loss_all.at[mine],
+                dst_ref=loss_all.at[mine],
+                send_sem=loss_send,
+                recv_sem=loss_recv,
+                device_id={"dp": target // seq_size, "seq": lax.rem(target, seq_size)},
+                device_id_type=MESH,
+            ).start()
+            return carry
+
+        lax.fori_loop(1, everyone, tell, 0)
+
+    if others:
+        steps = others * slab_count
+        lax.fori_loop(0, steps - 1, plain_step, 0)
+        gram_step(steps - 1, send_loss)
+    else:
+        send_loss()
 
     inv_sigma = stats[0]
     inv_length = stats[1]
@@ -339,29 +356,21 @@
     mean_scaled = (inv_length * gain_sum - cubed * stats[2]) * (1.0 / width)
     mean_product = cubed * (EPSILON / width)
 
-    for i in range(1, seq_size):
-        lseq(i).wait_recv()
-    image_sum = loss_seq[0]
-    for s in range(1, seq_size):
-        image_sum = image_sum + loss_seq[s]
-    loss_dp[image] = image_sum
-    for i in range(1, dp_size):
-        ldp(i).start()
-
     out_scale = inv_sigma * (tokens * math.sqrt(width))
     hat = hat_buf[...]
     scaled = (cot * (inv_length * cot_weight) - cubed * (hat * gain)) * gain
-    grad_ref[0] = ((scaled - mean_scaled - hat * mean_product) * out_scale).astype(jnp.bfloat16)
-
-    for i in range(1, dp_size):
-        ldp(i).wait_recv()
-    all_sum = loss_dp[0]
-    for s in range(1, dp_size):
-        all_sum = all_sum + loss_dp[s]
+    grad_buf[...] = ((scaled - mean_scaled - hat * mean_product) * out_scale).astype(jnp.bfloat16)
+    result = pltpu.make_async_copy(grad_buf, grad_ref.at[0], grad_sem)
+    result.start()
+
+    arrived = loss_all.at[pl.ds(0, everyone - 1)]
+    pltpu.make_async_copy(arrived, arrived, loss_recv).wait()
     loss_weight = width / (tokens * tokens)
-    image_ref[0, 0] = jnp.sum(image_sum) * loss_weight
-    mean_ref[0, 0] = jnp.sum(all_sum) * (loss_weight / dp_size)
-
+    image_ref[0, 0] = jnp.sum(loss_all[pl.ds(image * seq_size, seq_size)]) * loss_weight
+    mean_ref[0, 0] = jnp.sum(loss_all[...]) * (loss_weight / dp_size)
+
+    pltpu.make_async_copy(arrived, arrived, loss_send).wait()
+    result.wait()
     for t in range(2):
         whole(t).wait_send()
         for d in range(1, chips):
@@ -372,10 +381,6 @@
         for d in range(1, chips):
             fdirect(d, r).wait_send()
             frelay(d, r).wait_send()
-    for i in range(1, seq_size):
-        lseq(i).wait_send()
-    for i in range(1, dp_size):
-        ldp(i).wait_send()
 
 
 def local(seq_size, dp_size, queries, keys, values, stream, layer_scale, norm_gain, teacher_gram):
@@ -396,7 +401,7 @@
         ),
         in_specs=[any_space] * 7,
         out_specs=(
-            pl.BlockSpec(memory_space=pltpu.VMEM),
+            any_space,
             pl.BlockSpec(memory_space=pltpu.SMEM),
             pl.BlockSpec(memory_space=pltpu.SMEM),
         ),
@@ -413,8 +418,8 @@
             pltpu.VMEM((rows, width), jnp.float32),
             pltpu.VMEM((3, rows, 1), jnp.float32),
             pltpu.VMEM((8, rows), jnp.float32),
-            pltpu.VMEM((seq_size, 8, rows), jnp.float32),
-            pltpu.VMEM((dp_size, 8, rows), jnp.float32),
+            pltpu.VMEM((seq_size * dp_size, 1, rows), jnp.float32),
+            pltpu.VMEM((rows, width), jnp.bfloat16),
             dma((7,)),
             dma((2, others)),
             dma((2, others, chunk_count)),
@@ -428,10 +433,10 @@
             dma((slab_count,)),
             dma((others, slab_count)),
             dma((others, slab_count)),
-            dma((seq_size - 1,)),
-            dma((seq_size - 1,)),
-            dma((dp_size - 1,)),
-            dma((dp_size - 1,)),
+            dma,
+            dma,
+            dma,
+            pltpu.SemaphoreType.REGULAR((max(1, dp_size.bit_length()),)),
         ],
         compiler_params=pltpu.CompilerParams(
             collective_id=0, has_side_effects=True, vmem_limit_bytes=60 * 1024 * 1024

time: 61 us -> 58.1 us (0.952)
  Pallas kernels: 54.8 us -> 51.9 us
    pallas_call x1, Pallas kernels: 54.8 us -> 51.9 us  [local(): pl.pallas_call(functools.partial(kernel, seq_size, dp_size, chunk_count,...]
where the time goes in v2:
time: 58.1 us; the launch traced here: 57.9 us
  Pallas kernels  51.9 us (89%)
  between operations  4.1 us (7%)
  local copies, waits for them, and re-layouts  1.88 us (3%)
    pallas_call x1, Pallas kernels, local(): pl.pallas_call(functools.partial(kernel, seq_size, dp_size, chunk_count,...  51.9 us
    unnamed x1, local copies, waits for them, and re-layouts  1.88 us

profile of v2, /device:TPU:0, one launch (start us, length us, event | category | flops | bytes accessed | tf_op | source)
XLA Modules:
  0.0 57.9 jit_solution(13411474672673120773)
XLA Ops:
  0.6 51.9 %shard_map.94 = (bf16[1,128,2048]{2,1,0:T(8,128)(2,1)}, f32[1,1]{1,0:T(1,128)}, f32[1,1]{1,0:T(1,128)}) custom-call(bf16[1,128,2048]{2,1,0:T(8,128)(2,1)} %q_hbm.1, bf16[1,128,2048]{2,1,0:T(8,128)(2,1)} %k_hbm.1, bf16[1,128,2048]{2,1,0:T(8,128)(2,1)} %v_hbm.1, bf16[1,128,2048]{2,1,0:T(8,128)(2,1)} %stream_hbm.1, f32[1,2048]{1,0:T(1,128)} %bitcast.4, ...), custom_call_target="tpu_custom_call" | custom-call | tf_op jit(solution)/shard_map/pallas_call | solution.py:395
  52.5 1.9 %copy.13 = bf16[1,128,2048]{2,1,0:T(8,128)(2,1)} copy(bf16[1,128,2048]{2,1,0:T(8,128)(2,1)} %get-tuple-element.12) | data formatting | bytes 1048576

commit v3 on v2

--- a/solution.py
+++ b/solution.py
@@ -42,6 +42,7 @@
     hat_buf,
     feat_buf,
     cot_buf,
+    diff_buf,
     stats,
     loss_acc,
     loss_all,
@@ -183,7 +184,6 @@
         taught_t[s * rows : (s + 1) * rows, :] = jnp.transpose(
             teacher_buf[:, s * rows : (s + 1) * rows].astype(jnp.float32)
         )
-    cot_buf[...] = jnp.zeros_like(cot_buf)
     loss_acc[...] = jnp.zeros_like(loss_acc)
 
     heads = LANES // HEAD_DIM
@@ -292,31 +292,32 @@
         tile = lax.dot_general(block, feat_buf[me], NT, preferred_element_type=jnp.float32)
         differ = tile - taught_t[pl.ds(pl.multiple_of(s * rows + start, size), size), :]
         loss_acc[...] += jnp.sum((differ * differ).reshape(size // 8, 8, rows), axis=0)
-        return differ.astype(jnp.bfloat16)
-
-    def pull(differ, s, start, size):
-        block = feat_buf[s, pl.ds(start, size), :]
-        cot_buf[...] += lax.dot_general(differ, block, TN, preferred_element_type=jnp.float32)
-
-    pull(gram(me, 0, rows), me, 0, rows)
+        diff_buf[s, pl.ds(start, size), :] = differ.astype(jnp.bfloat16)
+
+    def pull(c):
+        both = pl.ds(c * CORES, CORES)
+        return lax.dot_general(
+            diff_buf[both].reshape(CORES * rows, rows),
+            feat_buf[both].reshape(CORES * rows, width),
+            TN,
+            preferred_element_type=jnp.float32,
+        )
+
+    gram(me, 0, rows)
     for r in range(slab_count):
         fpair(r).wait_recv()
-    pull(gram(partner, 0, rows), partner, 0, rows)
-
-    def gram_step(i, finish):
+    gram(partner, 0, rows)
+    cot_buf[...] = pull(chip)
+
+    def gram_step(i, carry):
         r = i // others
         d = lax.rem(i, others) + 1
         fdirect(d, r).wait_recv()
         frelay(d, r).start()
         start = pl.multiple_of(r * slab, slab)
-        pull(gram(source(d), start, slab), source(d), start, slab)
+        gram(source(d), start, slab)
         frelay(d, r).wait_recv()
-        last = gram(source_pair(d), start, slab)
-        finish()
-        pull(last, source_pair(d), start, slab)
-
-    def plain_step(i, carry):
-        gram_step(i, lambda: None)
+        gram(source_pair(d), start, slab)
         return carry
 
     everyone = seq_size * dp_size
@@ -339,12 +340,10 @@
 
         lax.fori_loop(1, everyone, tell, 0)
 
-    if others:
-        steps = others * slab_count
-        lax.fori_loop(0, steps - 1, plain_step, 0)
-        gram_step(steps - 1, send_loss)
-    else:
-        send_loss()
+    lax.fori_loop(0, others * slab_count, gram_step, 0)
+    send_loss()
+    for d in range(1, chips):
+        cot_buf[...] += pull(lax.rem(chip + d, chips))
 
     inv_sigma = stats[0]
     inv_length = stats[1]
@@ -416,6 +415,7 @@
             pltpu.VMEM((rows, width), jnp.float32),
             pltpu.VMEM((seq_size, rows, width), jnp.bfloat16),
             pltpu.VMEM((rows, width), jnp.float32),
+            pltpu.VMEM((seq_size, rows, rows), jnp.bfloat16),
             pltpu.VMEM((3, rows, 1), jnp.float32),
             pltpu.VMEM((8, rows), jnp.float32),
             pltpu.VMEM((seq_size * dp_size, 1, rows), jnp.float32),

time: 58.1 us -> 58.1 us (level)
  no operation moved by 1% of the time
where the time goes in v3:
time: 58.1 us; the launch traced here: 57.9 us
  Pallas kernels  51.9 us (89%)
  between operations  4.1 us (7%)
  local copies, waits for them, and re-layouts  1.88 us (3%)
    pallas_call x1, Pallas kernels, local(): pl.pallas_call(functools.partial(kernel, seq_size, dp_size, chunk_count,...  51.9 us
    unnamed x1, local copies, waits for them, and re-layouts  1.88 us

profile of v3, /device:TPU:0, one launch (start us, length us, event | category | flops | bytes accessed | tf_op | source)
XLA Modules:
  0.0 57.9 jit_solution(6282411524513187399)
XLA Ops:
  0.6 51.9 %shard_map.94 = (bf16[1,128,2048]{2,1,0:T(8,128)(2,1)}, f32[1,1]{1,0:T(1,128)}, f32[1,1]{1,0:T(1,128)}) custom-call(bf16[1,128,2048]{2,1,0:T(8,128)(2,1)} %q_hbm.1, bf16[1,128,2048]{2,1,0:T(8,128)(2,1)} %k_hbm.1, bf16[1,128,2048]{2,1,0:T(8,128)(2,1)} %v_hbm.1, bf16[1,128,2048]{2,1,0:T(8,128)(2,1)} %stream_hbm.1, f32[1,2048]{1,0:T(1,128)} %bitcast.4, ...), custom_call_target="tpu_custom_call" | custom-call | tf_op jit(solution)/shard_map/pallas_call | solution.py:394
  52.6 1.9 %copy.13 = bf16[1,128,2048]{2,1,0:T(8,128)(2,1)} copy(bf16[1,128,2048]{2,1,0:T(8,128)(2,1)} %get-tuple-element.12) | data formatting | bytes 1048576
